TPU v7x, 32 devices: a whole 2x2x4 slice. The times are simulated.
32 devices in a mesh: groups: 2 (over y), pages: 4 (over z), patches: 4 (over x, core).
Axes of the slice: x: 2, y: 2, z: 4, core: 2. Of those that a mesh axis runs over, the one named last changes fastest.
Arguments:
- queries: bfloat16 [16, 32, 128], P(('groups', 'pages'), 'patches'), parts along dimension 0, may hold values from -6 to 6
- gallery: bfloat16 [640, 1024, 128], P(('groups', 'pages'), 'patches'), parts along dimension 0, may hold values from -0.5 to 0.5
- page_rows: int32 [640], P('groups'), parts along dimension 0, may hold values from 0 to 319, as said below
- candidates: int32 [16, 32], P(('groups', 'pages')), parts along dimension 0, may hold values from 0 to 319, as said below
Outputs:
- scores: float32 [16, 32], P(('groups', 'pages')), parts along dimension 0
There are 2 independent parts, one for each index of `groups`. A program takes and returns all parts, laid end to end along the dimension named above; each array names one. Nothing has to cross between parts.
Inputs may be any that keep to these rules, and one draw needn't show every extreme that they name: A permutation: page id c is stored at row page_rows[c] of gallery, which lies on pages index page_rows[c] // 80. Each query's 32 page ids are distinct. The 2 queries of one pages index have at most 48 candidates stored on one pages index, and in every draw some pages index stores exactly 48 candidates of the queries of every pages index.
All inputs are finite; a program needn't handle non-finite values.
Results may differ from a plain program's by a relative error of at most 0.0003.
Values may be sent and summed in bfloat16 or wider, within the bound.
A program may use at most 64 MiB of HBM per device.

v0:
```python
import jax
import jax.numpy as jnp
from jax import lax
from jax.sharding import PartitionSpec as P

QT = 32
CAP = 48


def token_maxima(query_rows, gallery):
    page_count = gallery.shape[0]
    grouped = gallery.reshape(page_count // 8, 8, gallery.shape[1], gallery.shape[2])

    def per_block(block):
        sims = jnp.einsum("rd,bpd->brp", query_rows, block, preferred_element_type=jnp.float32)
        return jnp.max(sims, axis=2)

    result = lax.map(per_block, grouped)
    return result.reshape(page_count, query_rows.shape[0])


def slot_plan(storage, page_count, owner_count, query_count):
    flat_rows = storage.reshape(-1)
    holder = flat_rows // page_count
    local_page = flat_rows % page_count
    onehot = (holder[:, None] == jnp.arange(owner_count, dtype=jnp.int32)[None, :]).astype(
        jnp.int32
    )
    running = jnp.cumsum(onehot, axis=0) - onehot
    rank = jnp.sum(running * onehot, axis=1)
    query_ids = (
        lax.axis_index("pages") * query_count + jnp.arange(query_count, dtype=jnp.int32)[:, None]
    )
    query_ids = jnp.broadcast_to(query_ids, storage.shape).reshape(-1)
    codes = (
        jnp.full((owner_count, CAP), -1, jnp.int32)
        .at[holder, rank]
        .set(query_ids * page_count + local_page)
    )
    return (holder, rank, codes)


def body(queries, gallery, page_rows, candidates):
    query_count = queries.shape[0]
    page_count = gallery.shape[0]
    owner_count = lax.axis_size("pages")
    storage = jnp.take(page_rows, candidates, axis=0)
    local_tokens = lax.all_gather(queries, "patches", axis=1, tiled=True)
    shard_rows = lax.all_gather(local_tokens, "pages", axis=0, tiled=True)
    maxima = token_maxima(shard_rows.reshape(-1, shard_rows.shape[2]), gallery)
    part_count = lax.axis_size("patches")
    arrived = lax.all_to_all(maxima, "patches", split_axis=0, concat_axis=0, tiled=True)
    share_max = jnp.max(arrived.reshape(part_count, page_count // part_count, -1), axis=0)
    share_scores = jnp.mean(share_max.reshape(page_count // part_count, -1, QT), axis=2)
    page_scores = lax.all_gather(share_scores, "patches", axis=0, tiled=True)
    holder, rank, codes = slot_plan(storage, page_count, owner_count, query_count)
    incoming = lax.all_to_all(codes, "pages", split_axis=0, concat_axis=0, tiled=True)
    safe_codes = jnp.maximum(incoming, 0)
    picked = page_scores[safe_codes % page_count, safe_codes // page_count]
    picked = jnp.where(incoming >= 0, picked, 0.0)
    returned = lax.all_to_all(picked, "pages", split_axis=0, concat_axis=0, tiled=True)
    return returned[holder, rank].reshape(storage.shape)


def solution(mesh):
    in_specs = (
        P(("groups", "pages"), "patches", None),
        P(("groups", "pages"), "patches", None),
        P("groups"),
        P(("groups", "pages"), None),
    )
    out_specs = P(("groups", "pages"), None)
    return jax.shard_map(body, mesh=mesh, in_specs=in_specs, out_specs=out_specs, check_vma=False)
```

profile of v0, /device:TPU:0, one launch (start us, length us, event | category | flops | bytes accessed | tf_op | source)
XLA Modules:
  0.0 81.3 jit_solution(7018582230763072979)
XLA Ops:
  0.0 0.7 compare_select_fusion.3
  0.8 0.8 gather_fusion
  1.7 0.7 compare_and_fusion
  3.9 10.2 %scatter_fusion = s32[4,48]{1,0:T(4,128)} fusion(s32[4,48]{1,0:T(4,128)} %broadcast_in_dim.36, s32[64]{0:T(128)S(1)} %get-tuple-element.42, s32[64]{0:T(128)S(1)} %get-tuple-element.45), kind=kCustom, calls=%fused_computation.3 | custom fusion | bytes 1280 | tf_op jit(solution)/shard_map/scatter | solution.py:38
  14.1 6.3 %all-to-all-start = ((s32[4,1,48]{2,1,0:T(1,128)}), s32[4,1,48]{2,1,0:T(1,128)S(1)}, u32[]{:S(2)}, u32[]{:S(2)}) async-start(s32[4,1,48]{2,1,0:T(1,128)} %bitcast.6), calls=%async_computation | async-start | bytes 4096 | tf_op jit(solution)/shard_map/all_to_all | solution.py:57
  20.5 5.4 %all_gather.9 = bf16[2,32,128]{2,1,0:T(8,128)(2,1)S(1)} all-gather(bf16[2,8,128]{2,1,0:T(8,128)(2,1)} %param.6), channel_id=1, replica_groups=mesh['groups'=2,'pages'=4,'patches'=4] {'patches'}, dimensions={1}, use_global_device_ids=true | all-gather | bytes 20480 | tf_op jit(solution)/shard_map/all_gather | solution.py:48
  25.9 13.7 %all_gather.10 = bf16[8,32,128]{2,1,0:T(8,128)(2,1)S(1)} all-gather(bf16[2,32,128]{2,1,0:T(8,128)(2,1)S(1)} %all_gather.9), channel_id=1, replica_groups=mesh['groups'=2,'pages'=4,'patches'=4] {'pages'}, dimensions={0}, use_global_device_ids=true | all-gather | bytes 81920 | tf_op jit(solution)/shard_map/all_gather | solution.py:49
  39.5 15.2 %while.10 = (s32[]{:T(128)}, f32[10,8,256]{2,1,0:T(8,128)S(1)}, bf16[10,8,256,128]{3,2,1,0:T(8,128)(2,1)}, bf16[256,128]{1,0:T(8,128)(2,1)S(1)}, s32[]{:T(128)}) while((s32[]{:T(128)}, f32[10,8,256]{2,1,0:T(8,128)S(1)}, bf16[10,8,256,128]{3,2,1,0:T(8,128)(2,1)}, bf16[256,128]{1,0:T(8,128)(2,1)S(1)}, s32[]{:T(128)}) %tuple.28), condition=%wide.region_5.6_spmd, body=%wide.region_3.5_spmd.sunk | while | flops 134739968 | bytes 614477 | solution.py:18
  39.5 1.5 %convolution_reduce_fusion.2 = f32[8,256]{1,0:T(8,128)S(1)} fusion(bf16[10,8,256,128]{3,2,1,0:T(8,128)(2,1)} %get-tuple-element.84, s32[]{:T(128)S(6)} %copy.20, bf16[256,128]{1,0:T(8,128)(2,1)S(1)} %get-tuple-element.85), kind=kOutput, calls=%fused_computation.4.clone.1 | convolution fusion | flops 134739968 | bytes 598020 | tf_op jit(solution)/shard_map/while/body/eval_jaxpr/rd,bpd->brp/dot_general | solution.py:15
  41.1 1.5 %convolution_reduce_fusion.2 = f32[8,256]{1,0:T(8,128)S(1)} fusion(bf16[10,8,256,128]{3,2,1,0:T(8,128)(2,1)} %get-tuple-element.84, s32[]{:T(128)S(6)} %copy.20, bf16[256,128]{1,0:T(8,128)(2,1)S(1)} %get-tuple-element.85), kind=kOutput, calls=%fused_computation.4.clone.1 | convolution fusion | flops 134739968 | bytes 598020 | tf_op jit(solution)/shard_map/while/body/eval_jaxpr/rd,bpd->brp/dot_general | solution.py:15
  42.6 1.5 %convolution_reduce_fusion.2 = f32[8,256]{1,0:T(8,128)S(1)} fusion(bf16[10,8,256,128]{3,2,1,0:T(8,128)(2,1)} %get-tuple-element.84, s32[]{:T(128)S(6)} %copy.20, bf16[256,128]{1,0:T(8,128)(2,1)S(1)} %get-tuple-element.85), kind=kOutput, calls=%fused_computation.4.clone.1 | convolution fusion | flops 134739968 | bytes 598020 | tf_op jit(solution)/shard_map/while/body/eval_jaxpr/rd,bpd->brp/dot_general | solution.py:15
  44.1 1.5 %convolution_reduce_fusion.2 = f32[8,256]{1,0:T(8,128)S(1)} fusion(bf16[10,8,256,128]{3,2,1,0:T(8,128)(2,1)} %get-tuple-element.84, s32[]{:T(128)S(6)} %copy.20, bf16[256,128]{1,0:T(8,128)(2,1)S(1)} %get-tuple-element.85), kind=kOutput, calls=%fused_computation.4.clone.1 | convolution fusion | flops 134739968 | bytes 598020 | tf_op jit(solution)/shard_map/while/body/eval_jaxpr/rd,bpd->brp/dot_general | solution.py:15
  45.6 1.5 %convolution_reduce_fusion.2 = f32[8,256]{1,0:T(8,128)S(1)} fusion(bf16[10,8,256,128]{3,2,1,0:T(8,128)(2,1)} %get-tuple-element.84, s32[]{:T(128)S(6)} %copy.20, bf16[256,128]{1,0:T(8,128)(2,1)S(1)} %get-tuple-element.85), kind=kOutput, calls=%fused_computation.4.clone.1 | convolution fusion | flops 134739968 | bytes 598020 | tf_op jit(solution)/shard_map/while/body/eval_jaxpr/rd,bpd->brp/dot_general | solution.py:15
  47.2 1.5 %convolution_reduce_fusion.2 = f32[8,256]{1,0:T(8,128)S(1)} fusion(bf16[10,8,256,128]{3,2,1,0:T(8,128)(2,1)} %get-tuple-element.84, s32[]{:T(128)S(6)} %copy.20, bf16[256,128]{1,0:T(8,128)(2,1)S(1)} %get-tuple-element.85), kind=kOutput, calls=%fused_computation.4.clone.1 | convolution fusion | flops 134739968 | bytes 598020 | tf_op jit(solution)/shard_map/while/body/eval_jaxpr/rd,bpd->brp/dot_general | solution.py:15
  48.7 1.5 %convolution_reduce_fusion.2 = f32[8,256]{1,0:T(8,128)S(1)} fusion(bf16[10,8,256,128]{3,2,1,0:T(8,128)(2,1)} %get-tuple-element.84, s32[]{:T(128)S(6)} %copy.20, bf16[256,128]{1,0:T(8,128)(2,1)S(1)} %get-tuple-element.85), kind=kOutput, calls=%fused_computation.4.clone.1 | convolution fusion | flops 134739968 | bytes 598020 | tf_op jit(solution)/shard_map/while/body/eval_jaxpr/rd,bpd->brp/dot_general | solution.py:15
  50.2 1.5 %convolution_reduce_fusion.2 = f32[8,256]{1,0:T(8,128)S(1)} fusion(bf16[10,8,256,128]{3,2,1,0:T(8,128)(2,1)} %get-tuple-element.84, s32[]{:T(128)S(6)} %copy.20, bf16[256,128]{1,0:T(8,128)(2,1)S(1)} %get-tuple-element.85), kind=kOutput, calls=%fused_computation.4.clone.1 | convolution fusion | flops 134739968 | bytes 598020 | tf_op jit(solution)/shard_map/while/body/eval_jaxpr/rd,bpd->brp/dot_general | solution.py:15
  51.7 1.5 %convolution_reduce_fusion.2 = f32[8,256]{1,0:T(8,128)S(1)} fusion(bf16[10,8,256,128]{3,2,1,0:T(8,128)(2,1)} %get-tuple-element.84, s32[]{:T(128)S(6)} %copy.20, bf16[256,128]{1,0:T(8,128)(2,1)S(1)} %get-tuple-element.85), kind=kOutput, calls=%fused_computation.4.clone.1 | convolution fusion | flops 134739968 | bytes 598020 | tf_op jit(solution)/shard_map/while/body/eval_jaxpr/rd,bpd->brp/dot_general | solution.py:15
  53.3 1.5 %convolution_reduce_fusion.2 = f32[8,256]{1,0:T(8,128)S(1)} fusion(bf16[10,8,256,128]{3,2,1,0:T(8,128)(2,1)} %get-tuple-element.84, s32[]{:T(128)S(6)} %copy.20, bf16[256,128]{1,0:T(8,128)(2,1)S(1)} %get-tuple-element.85), kind=kOutput, calls=%fused_computation.4.clone.1 | convolution fusion | flops 134739968 | bytes 598020 | tf_op jit(solution)/shard_map/while/body/eval_jaxpr/rd,bpd->brp/dot_general | solution.py:15
  55.4 3.3 %all-to-all-start.1 = ((f32[4,20,256]{2,1,0:T(8,128)}), f32[4,20,256]{2,1,0:T(8,128)S(1)}, u32[]{:S(2)}, u32[]{:S(2)}) async-start(f32[4,20,256]{2,1,0:T(8,128)} %all_to_all.20), calls=%async_computation.1 | async-start | bytes 196608 | tf_op jit(solution)/shard_map/all_to_all | solution.py:52
  59.1 3.9 %all-to-all-done.1 = f32[4,20,256]{2,1,0:T(8,128)S(1)} async-done(((f32[4,20,256]{2,1,0:T(8,128)}), f32[4,20,256]{2,1,0:T(8,128)S(1)}, u32[]{:S(2)}, u32[]{:S(2)}) %all-to-all-start.1) | async-done | bytes 81952 | tf_op jit(solution)/shard_map/all_to_all | solution.py:52
  63.3 5.2 %all-gather = f32[4,20,8]{1,2,0:T(8,128)S(1)} all-gather(f32[1,20,8]{1,2,0:T(8,128)S(1)} %copy.12), channel_id=1, replica_groups=mesh['groups'=2,'pages'=4,'patches'=4] {'patches'}, dimensions={0}, use_global_device_ids=true | all-gather | bytes 3200 | tf_op jit(solution)/shard_map/all_gather | solution.py:55
  68.6 1.2 %gather_fusion.1 = f32[192]{0:T(256)S(1)} fusion(f32[80,8]{0,1:T(8,128)S(1)} %reshape.242, s32[192]{0:T(256)S(1)} %reshape.220), kind=kCustom, calls=%fused_computation.1 | custom fusion | bytes 3072 | tf_op jit(solution)/shard_map/gather | solution.py:59
  69.8 9.9 %all_to_all.27 = f32[4,1,48]{2,1,0:T(1,128)S(1)} all-to-all(f32[4,1,48]{2,1,0:T(1,128)S(1)} %compare_select_fusion), channel_id=1, replica_groups=mesh['groups'=2,'pages'=4,'patches'=4] {'pages'}, dimensions={0} | all-to-all | bytes 1536 | tf_op jit(solution)/shard_map/all_to_all | solution.py:61
  79.7 0.9 %gather_fusion.2 = f32[64]{0:T(128)S(1)} fusion(f32[4,48]{1,0:T(4,128)S(1)} %bitcast.60, s32[64]{0:T(128)S(1)} %get-tuple-element.41), kind=kCustom, calls=%fused_computation.2 | custom fusion | bytes 1024 | tf_op jit(solution)/shard_map/gather | solution.py:62
  (47 shorter events, 3.9 us)
Async XLA Ops:
  0.0 0.8 copy-start
  14.1 41.3 %all-to-all-start = ((s32[4,1,48]{2,1,0:T(1,128)}), s32[4,1,48]{2,1,0:T(1,128)S(1)}, u32[]{:S(2)}, u32[]{:S(2)}) async-start(s32[4,1,48]{2,1,0:T(1,128)} %bitcast.6), calls=%async_computation | async-start | bytes 4096 | tf_op jit(solution)/shard_map/all_to_all | solution.py:57
  55.4 7.6 %all-to-all-start.1 = ((f32[4,20,256]{2,1,0:T(8,128)}), f32[4,20,256]{2,1,0:T(8,128)S(1)}, u32[]{:S(2)}, u32[]{:S(2)}) async-start(f32[4,20,256]{2,1,0:T(8,128)} %all_to_all.20), calls=%async_computation.1 | async-start | bytes 196608 | tf_op jit(solution)/shard_map/all_to_all | solution.py:52
where the time goes:
time: 82.3 us; the launch traced here: 81.3 us
  blocking collectives  34.2 us (42%)
  local copies, waits for them, and re-layouts  16.2 us (20%)
  matrix products  14.9 us (18%)
  starting transfers between devices  9.65 us (12%)
  waiting for transfers between devices  3.93 us (5%)
  other arithmetic  2.15 us (3%)
    dot_general x10, matrix products, per_block(): jnp.einsum('rd,bpd->brp', query_rows, block, preferred_element_type=jnp.f...  14.9 us
    all_gather x1, blocking collectives, body(): shard_rows = lax.all_gather(local_tokens, 'pages', axis=0, tiled=True)  13.7 us
    scatter x1, local copies, waits for them, and re-layouts, slot_plan(): codes = jnp.full((owner_count, CAP), -1, jnp.int32).at[holder, rank].set(...  10.2 us
    all_to_all x1, blocking collectives, body(): lax.all_to_all(picked, 'pages', split_axis=0, concat_axis=0, tiled=True)  9.92 us
    all_to_all x1, starting transfers between devices, body(): lax.all_to_all(codes, 'pages', split_axis=0, concat_axis=0, tiled=True)  6.35 us
    all_gather x1, blocking collectives, body(): local_tokens = lax.all_gather(queries, 'patches', axis=1, tiled=True)  5.37 us
    all_gather x1, blocking collectives, body(): page_scores = lax.all_gather(share_scores, 'patches', axis=0, tiled=True)  5.19 us
    all_to_all x1, waiting for transfers between devices, body(): lax.all_to_all(maxima, 'patches', split_axis=0, concat_axis=0, tiled=True)  3.93 us
  transfers between devices with their start and end apart: 2, of which 1 were waited for; matrix products, arithmetic and copies ran while one was open for 19% of the time, Pallas kernels for 0%

commit v1 on v0

--- a/solution.py
+++ b/solution.py
@@ -45,7 +45,7 @@
     page_count = gallery.shape[0]
     owner_count = lax.axis_size("pages")
     storage = jnp.take(page_rows, candidates, axis=0)
-    local_tokens = lax.all_gather(queries, "patches", axis=1, tiled=True)
+    local_tokens = jnp.concatenate(lax.all_gather(queries, "patches"), axis=1)
     shard_rows = lax.all_gather(local_tokens, "pages", axis=0, tiled=True)
     maxima = token_maxima(shard_rows.reshape(-1, shard_rows.shape[2]), gallery)
     part_count = lax.axis_size("patches")

time: 82.3 us -> 82.2 us (level)
  no operation moved by 1% of the time
where the time goes in v1:
time: 82.2 us; the launch traced here: 81.2 us
  blocking collectives  34.1 us (41%)
  local copies, waits for them, and re-layouts  16.2 us (20%)
  matrix products  14.9 us (18%)
  starting transfers between devices  9.65 us (12%)
  waiting for transfers between devices  3.93 us (5%)
  other arithmetic  2.15 us (3%)
    dot_general x10, matrix products, per_block(): jnp.einsum('rd,bpd->brp', query_rows, block, preferred_element_type=jnp.f...  14.9 us
    all_gather x1, blocking collectives, body(): shard_rows = lax.all_gather(local_tokens, 'pages', axis=0, tiled=True)  13.7 us
    scatter x1, local copies, waits for them, and re-layouts, slot_plan(): codes = jnp.full((owner_count, CAP), -1, jnp.int32).at[holder, rank].set(...  10.2 us
    all_to_all x1, blocking collectives, body(): lax.all_to_all(picked, 'pages', split_axis=0, concat_axis=0, tiled=True)  9.9 us
    all_to_all x1, starting transfers between devices, body(): lax.all_to_all(codes, 'pages', split_axis=0, concat_axis=0, tiled=True)  6.35 us
    all_gather x1, blocking collectives, body(): local_tokens = jnp.concatenate(lax.all_gather(queries, 'patches'), axis=1)  5.32 us
    all_gather x1, blocking collectives, body(): page_scores = lax.all_gather(share_scores, 'patches', axis=0, tiled=True)  5.19 us
    all_to_all x1, waiting for transfers between devices, body(): lax.all_to_all(maxima, 'patches', split_axis=0, concat_axis=0, tiled=True)  3.93 us
  transfers between devices with their start and end apart: 2, of which 1 were waited for; matrix products, arithmetic and copies ran while one was open for 19% of the time, Pallas kernels for 0%

profile of v1, /device:TPU:0, one launch (start us, length us, event | category | flops | bytes accessed | tf_op | source)
XLA Modules:
  0.0 81.2 jit_solution(6753608963993093545)
XLA Ops:
  0.0 0.7 compare_select_fusion.3
  0.8 0.8 gather_fusion
  1.7 0.7 compare_and_fusion
  3.9 10.2 %scatter_fusion = s32[4,48]{1,0:T(4,128)} fusion(s32[4,48]{1,0:T(4,128)} %broadcast_in_dim.36, s32[64]{0:T(128)S(1)} %get-tuple-element.42, s32[64]{0:T(128)S(1)} %get-tuple-element.45), kind=kCustom, calls=%fused_computation.3 | custom fusion | bytes 1280 | tf_op jit(solution)/shard_map/scatter | solution.py:38
  14.1 6.3 %all-to-all-start = ((s32[4,1,48]{2,1,0:T(1,128)}), s32[4,1,48]{2,1,0:T(1,128)S(1)}, u32[]{:S(2)}, u32[]{:S(2)}) async-start(s32[4,1,48]{2,1,0:T(1,128)} %bitcast.6), calls=%async_computation | async-start | bytes 4096 | tf_op jit(solution)/shard_map/all_to_all | solution.py:57
  20.5 5.3 %all-gather = bf16[8,8,128]{2,1,0:T(8,128)(2,1)S(1)} all-gather(bf16[2,8,128]{2,1,0:T(8,128)(2,1)} %param.6), channel_id=2, replica_groups=mesh['groups'=2,'pages'=4,'patches'=4] {'patches'}, dimensions={0}, use_global_device_ids=true | all-gather | bytes 20480 | tf_op jit(solution)/shard_map/all_gather | solution.py:48
  25.8 13.7 %all_gather.14 = bf16[8,32,128]{2,1,0:T(8,128)(2,1)S(1)} all-gather(bf16[2,32,128]{2,1,0:T(8,128)(2,1)S(1)} %bitcast.68), channel_id=1, replica_groups=mesh['groups'=2,'pages'=4,'patches'=4] {'pages'}, dimensions={0}, use_global_device_ids=true | all-gather | bytes 81920 | tf_op jit(solution)/shard_map/all_gather | solution.py:49
  39.5 15.2 %while.10 = (s32[]{:T(128)}, f32[10,8,256]{2,1,0:T(8,128)S(1)}, bf16[10,8,256,128]{3,2,1,0:T(8,128)(2,1)}, bf16[256,128]{1,0:T(8,128)(2,1)S(1)}, s32[]{:T(128)}) while((s32[]{:T(128)}, f32[10,8,256]{2,1,0:T(8,128)S(1)}, bf16[10,8,256,128]{3,2,1,0:T(8,128)(2,1)}, bf16[256,128]{1,0:T(8,128)(2,1)S(1)}, s32[]{:T(128)}) %tuple.28), condition=%wide.region_5.6_spmd, body=%wide.region_3.5_spmd.sunk | while | flops 134739968 | bytes 614477 | solution.py:18
  39.5 1.5 %convolution_reduce_fusion.2 = f32[8,256]{1,0:T(8,128)S(1)} fusion(bf16[10,8,256,128]{3,2,1,0:T(8,128)(2,1)} %get-tuple-element.84, s32[]{:T(128)S(6)} %copy.27, bf16[256,128]{1,0:T(8,128)(2,1)S(1)} %get-tuple-element.85), kind=kOutput, calls=%fused_computation.4.clone.1 | convolution fusion | flops 134739968 | bytes 598020 | tf_op jit(solution)/shard_map/while/body/eval_jaxpr/rd,bpd->brp/dot_general | solution.py:15
  41.0 1.5 %convolution_reduce_fusion.2 = f32[8,256]{1,0:T(8,128)S(1)} fusion(bf16[10,8,256,128]{3,2,1,0:T(8,128)(2,1)} %get-tuple-element.84, s32[]{:T(128)S(6)} %copy.27, bf16[256,128]{1,0:T(8,128)(2,1)S(1)} %get-tuple-element.85), kind=kOutput, calls=%fused_computation.4.clone.1 | convolution fusion | flops 134739968 | bytes 598020 | tf_op jit(solution)/shard_map/while/body/eval_jaxpr/rd,bpd->brp/dot_general | solution.py:15
  42.5 1.5 %convolution_reduce_fusion.2 = f32[8,256]{1,0:T(8,128)S(1)} fusion(bf16[10,8,256,128]{3,2,1,0:T(8,128)(2,1)} %get-tuple-element.84, s32[]{:T(128)S(6)} %copy.27, bf16[256,128]{1,0:T(8,128)(2,1)S(1)} %get-tuple-element.85), kind=kOutput, calls=%fused_computation.4.clone.1 | convolution fusion | flops 134739968 | bytes 598020 | tf_op jit(solution)/shard_map/while/body/eval_jaxpr/rd,bpd->brp/dot_general | solution.py:15
  44.1 1.5 %convolution_reduce_fusion.2 = f32[8,256]{1,0:T(8,128)S(1)} fusion(bf16[10,8,256,128]{3,2,1,0:T(8,128)(2,1)} %get-tuple-element.84, s32[]{:T(128)S(6)} %copy.27, bf16[256,128]{1,0:T(8,128)(2,1)S(1)} %get-tuple-element.85), kind=kOutput, calls=%fused_computation.4.clone.1 | convolution fusion | flops 134739968 | bytes 598020 | tf_op jit(solution)/shard_map/while/body/eval_jaxpr/rd,bpd->brp/dot_general | solution.py:15
  45.6 1.5 %convolution_reduce_fusion.2 = f32[8,256]{1,0:T(8,128)S(1)} fusion(bf16[10,8,256,128]{3,2,1,0:T(8,128)(2,1)} %get-tuple-element.84, s32[]{:T(128)S(6)} %copy.27, bf16[256,128]{1,0:T(8,128)(2,1)S(1)} %get-tuple-element.85), kind=kOutput, calls=%fused_computation.4.clone.1 | convolution fusion | flops 134739968 | bytes 598020 | tf_op jit(solution)/shard_map/while/body/eval_jaxpr/rd,bpd->brp/dot_general | solution.py:15
  47.1 1.5 %convolution_reduce_fusion.2 = f32[8,256]{1,0:T(8,128)S(1)} fusion(bf16[10,8,256,128]{3,2,1,0:T(8,128)(2,1)} %get-tuple-element.84, s32[]{:T(128)S(6)} %copy.27, bf16[256,128]{1,0:T(8,128)(2,1)S(1)} %get-tuple-element.85), kind=kOutput, calls=%fused_computation.4.clone.1 | convolution fusion | flops 134739968 | bytes 598020 | tf_op jit(solution)/shard_map/while/body/eval_jaxpr/rd,bpd->brp/dot_general | solution.py:15
  48.6 1.5 %convolution_reduce_fusion.2 = f32[8,256]{1,0:T(8,128)S(1)} fusion(bf16[10,8,256,128]{3,2,1,0:T(8,128)(2,1)} %get-tuple-element.84, s32[]{:T(128)S(6)} %copy.27, bf16[256,128]{1,0:T(8,128)(2,1)S(1)} %get-tuple-element.85), kind=kOutput, calls=%fused_computation.4.clone.1 | convolution fusion | flops 134739968 | bytes 598020 | tf_op jit(solution)/shard_map/while/body/eval_jaxpr/rd,bpd->brp/dot_general | solution.py:15
  50.2 1.5 %convolution_reduce_fusion.2 = f32[8,256]{1,0:T(8,128)S(1)} fusion(bf16[10,8,256,128]{3,2,1,0:T(8,128)(2,1)} %get-tuple-element.84, s32[]{:T(128)S(6)} %copy.27, bf16[256,128]{1,0:T(8,128)(2,1)S(1)} %get-tuple-element.85), kind=kOutput, calls=%fused_computation.4.clone.1 | convolution fusion | flops 134739968 | bytes 598020 | tf_op jit(solution)/shard_map/while/body/eval_jaxpr/rd,bpd->brp/dot_general | solution.py:15
  51.7 1.5 %convolution_reduce_fusion.2 = f32[8,256]{1,0:T(8,128)S(1)} fusion(bf16[10,8,256,128]{3,2,1,0:T(8,128)(2,1)} %get-tuple-element.84, s32[]{:T(128)S(6)} %copy.27, bf16[256,128]{1,0:T(8,128)(2,1)S(1)} %get-tuple-element.85), kind=kOutput, calls=%fused_computation.4.clone.1 | convolution fusion | flops 134739968 | bytes 598020 | tf_op jit(solution)/shard_map/while/body/eval_jaxpr/rd,bpd->brp/dot_general | solution.py:15
  53.2 1.5 %convolution_reduce_fusion.2 = f32[8,256]{1,0:T(8,128)S(1)} fusion(bf16[10,8,256,128]{3,2,1,0:T(8,128)(2,1)} %get-tuple-element.84, s32[]{:T(128)S(6)} %copy.27, bf16[256,128]{1,0:T(8,128)(2,1)S(1)} %get-tuple-element.85), kind=kOutput, calls=%fused_computation.4.clone.1 | convolution fusion | flops 134739968 | bytes 598020 | tf_op jit(solution)/shard_map/while/body/eval_jaxpr/rd,bpd->brp/dot_general | solution.py:15
  55.4 3.3 %all-to-all-start.1 = ((f32[4,20,256]{2,1,0:T(8,128)}), f32[4,20,256]{2,1,0:T(8,128)S(1)}, u32[]{:S(2)}, u32[]{:S(2)}) async-start(f32[4,20,256]{2,1,0:T(8,128)} %all_to_all.20), calls=%async_computation.1 | async-start | bytes 196608 | tf_op jit(solution)/shard_map/all_to_all | solution.py:52
  59.0 3.9 %all-to-all-done.1 = f32[4,20,256]{2,1,0:T(8,128)S(1)} async-done(((f32[4,20,256]{2,1,0:T(8,128)}), f32[4,20,256]{2,1,0:T(8,128)S(1)}, u32[]{:S(2)}, u32[]{:S(2)}) %all-to-all-start.1) | async-done | bytes 81952 | tf_op jit(solution)/shard_map/all_to_all | solution.py:52
  63.2 5.2 %all-gather.1 = f32[4,20,8]{1,2,0:T(8,128)S(1)} all-gather(f32[1,20,8]{1,2,0:T(8,128)S(1)} %copy.17), channel_id=1, replica_groups=mesh['groups'=2,'pages'=4,'patches'=4] {'patches'}, dimensions={0}, use_global_device_ids=true | all-gather | bytes 3200 | tf_op jit(solution)/shard_map/all_gather | solution.py:55
  68.5 1.2 %gather_fusion.1 = f32[192]{0:T(256)S(1)} fusion(f32[80,8]{0,1:T(8,128)S(1)} %reshape.251, s32[192]{0:T(256)S(1)} %reshape.228), kind=kCustom, calls=%fused_computation.1 | custom fusion | bytes 3072 | tf_op jit(solution)/shard_map/gather | solution.py:59
  69.8 9.9 %all_to_all.27 = f32[4,1,48]{2,1,0:T(1,128)S(1)} all-to-all(f32[4,1,48]{2,1,0:T(1,128)S(1)} %compare_select_fusion), channel_id=1, replica_groups=mesh['groups'=2,'pages'=4,'patches'=4] {'pages'}, dimensions={0} | all-to-all | bytes 1536 | tf_op jit(solution)/shard_map/all_to_all | solution.py:61
  79.7 0.9 %gather_fusion.2 = f32[64]{0:T(128)S(1)} fusion(f32[4,48]{1,0:T(4,128)S(1)} %bitcast.66, s32[64]{0:T(128)S(1)} %get-tuple-element.41), kind=kCustom, calls=%fused_computation.2 | custom fusion | bytes 1024 | tf_op jit(solution)/shard_map/gather | solution.py:62
  (48 shorter events, 3.9 us)
Async XLA Ops:
  0.0 0.8 copy-start
  14.1 41.2 %all-to-all-start = ((s32[4,1,48]{2,1,0:T(1,128)}), s32[4,1,48]{2,1,0:T(1,128)S(1)}, u32[]{:S(2)}, u32[]{:S(2)}) async-start(s32[4,1,48]{2,1,0:T(1,128)} %bitcast.6), calls=%async_computation | async-start | bytes 4096 | tf_op jit(solution)/shard_map/all_to_all | solution.py:57
  55.4 7.6 %all-to-all-start.1 = ((f32[4,20,256]{2,1,0:T(8,128)}), f32[4,20,256]{2,1,0:T(8,128)S(1)}, u32[]{:S(2)}, u32[]{:S(2)}) async-start(f32[4,20,256]{2,1,0:T(8,128)} %all_to_all.20), calls=%async_computation.1 | async-start | bytes 196608 | tf_op jit(solution)/shard_map/all_to_all | solution.py:52
